TPU v7x, 32 devices: a whole 2x2x4 slice. The times are simulated.
32 devices in a mesh: blk: 16 (over z, y, core), tile: 2 (over x).
Axes of the slice: x: 2, y: 2, z: 4, core: 2. Of those that a mesh axis runs over, the one named last changes fastest.
Arguments:
- positions: float32 [3, 2048], P(None, ('blk', 'tile')), as said below
- noise_vectors: float32 [3, 32, 2048], P(None, None, ('blk', 'tile')), may hold values from -6 to 6
- spectrum_bounds: float32 [2], replicated, as said below
Outputs:
- displacement: float32 [3, 32, 2048], P(None, None, ('blk', 'tile'))
- images: float32 [2, 3, 32, 2048], P(None, None, None, ('blk', 'tile'))
Inputs may be any that keep to these rules, and one draw needn't show every extreme that they name: `positions`: coordinates lie in a cube whose edge is the cube root of 41.9 * 2048; particle n's third coordinate lies between n and n + 1 times that edge divided by 2048. `spectrum_bounds`: the first entry lies between 0.15 and 0.35; the second exceeds 50 times the first.
All inputs are finite; a program needn't handle non-finite values.
Results may differ from a plain program's by a relative error of at most 0.0003.
Values sent between devices are 32-bit elements; how exact they have to be, the bound alone decides.
No kernel may reach another device: no remote copies, remote signals or barrier semaphores. Data moves between devices by JAX's collectives and lax.ppermute only.
A program may use at most 64 MiB of HBM per device.

v0:
```python
import math
import jax
import jax.numpy as jnp
from jax import lax
from jax.sharding import PartitionSpec as P

soft_core = 1e-06
node_count = 32


def from_partner(block, axis, apart):
    count = lax.axis_size(axis)
    route = []
    for low in range(count):
        high = low | 1 << apart
        if high != low and high < count:
            route += [(low, high), (high, low)]
    return lax.ppermute(block, axis, route)


def kernel(targets, sources):
    offset = targets[:, :, None] - sources[:, None, :]
    squared = jnp.sum(offset * offset, axis=0) + soft_core
    distance = jnp.sqrt(squared)
    inverse = 1.0 / distance
    cubed = inverse * inverse * inverse
    intersection = distance < 2.0
    scalar_part = jnp.where(intersection, 1.0 - 0.28125 * distance, 0.75 * inverse + 0.5 * cubed)
    dyadic_part = jnp.where(
        intersection, 0.09375 * inverse, 0.75 * cubed - 1.5 * cubed * inverse * inverse
    )
    identity = jnp.eye(3, dtype=targets.dtype)
    return (
        identity[:, :, None, None] * scalar_part[None, None]
        + dyadic_part[None, None] * offset[:, None] * offset[None, :]
    )


def contract(tensor, vectors):
    return jnp.einsum("abij,bkj->aki", tensor, vectors, precision=lax.Precision.HIGHEST)


def weights_from(bounds):
    lowest = bounds[0]
    highest = bounds[1]
    center = 0.5 * (highest + lowest)
    spread = 0.5 * (highest - lowest)
    angles = math.pi * (jnp.arange(node_count, dtype=bounds.dtype) + 0.5) / node_count
    samples = jnp.sqrt(center + spread * jnp.cos(angles))
    weights = [2.0 / node_count * jnp.sum(samples * jnp.cos(order * angles)) for order in range(3)]
    return (center, spread, weights)


def apply_blocks(targets, incoming):
    return contract(kernel(targets, incoming[:, 0, :]), incoming[:, 1:, :])


def grid_product(packed, positions):
    half_bits = (lax.axis_size("blk").bit_length() - 1) // 2
    block_number = lax.axis_index("blk")
    sources = lax.all_gather(packed, "tile", axis=2, tiled=True)
    for bit_number in range(half_bits, 2 * half_bits):
        partner = from_partner(sources, "blk", bit_number)
        sources = jnp.concatenate([sources, partner], axis=2)
    targets = positions
    for bit_number in range(half_bits):
        partner = from_partner(targets, "blk", bit_number)
        own_bit = block_number // (1 << bit_number) % 2
        targets = jnp.where(
            own_bit == 1,
            jnp.concatenate([partner, targets], axis=1),
            jnp.concatenate([targets, partner], axis=1),
        )
    partial_value = apply_blocks(targets, sources)
    for bit_number in reversed(range(half_bits)):
        half_width = partial_value.shape[2] // 2
        own_bit = block_number // (1 << bit_number) % 2
        kept_half = lax.dynamic_slice_in_dim(partial_value, own_bit * half_width, half_width, 2)
        sent_half = lax.dynamic_slice_in_dim(
            partial_value, (1 - own_bit) * half_width, half_width, 2
        )
        partial_value = kept_half + from_partner(sent_half, "blk", bit_number)
    return partial_value


def mobility(vectors, positions):
    packed = jnp.concatenate([positions[:, None, :], vectors], axis=1)
    return grid_product(packed, positions)


def body(positions, noise_vectors, spectrum_bounds):
    center, spread, weights = weights_from(spectrum_bounds)
    first_image = mobility(noise_vectors, positions)
    linear_term = (first_image - center * noise_vectors) / spread
    second_image = mobility(linear_term, positions)
    quadratic_term = 2.0 * (second_image - center * linear_term) / spread - noise_vectors
    displacement = (
        0.5 * weights[0] * noise_vectors + weights[1] * linear_term + weights[2] * quadratic_term
    )
    return (displacement, jnp.stack([first_image, second_image]))


def solution(mesh):
    return jax.shard_map(
        body,
        mesh=mesh,
        in_specs=(P(None, ("blk", "tile")), P(None, None, ("blk", "tile")), P()),
        out_specs=(P(None, None, ("blk", "tile")), P(None, None, None, ("blk", "tile"))),
        check_vma=False,
    )
```

profile of v0, /device:TPU:1, one launch (start us, length us, event | category | flops | bytes accessed | tf_op | source)
XLA Modules:
  0.0 68.6 jit_solution(18296448946351239026)
XLA Ops:
  0.7 0.7 broadcast_in_dim.2
  1.4 0.8 %pad_maximum_fusion.6 = f32[3,33,64]{2,1,0:T(8,128)S(1)} fusion(f32[3,1,64]{2,1,0:T(1,128)S(1)} %broadcast_in_dim.2, f32[3,32,64]{2,1,0:T(8,128)} %param.4), kind=kLoop, calls=%fused_computation.52 | loop fusion | flops 6336 | bytes 50688 | tf_op jit(solution)/shard_map/concatenate | solution.py:87
  2.3 7.2 %all_gather.6 = f32[3,33,128]{1,0,2:T(4,128)S(1)} all-gather(f32[3,33,64]{1,0,2:T(4,128)S(1)} %copy.14), channel_id=1, replica_groups=mesh['blk'=16,'tile'=2] {'tile'}, dimensions={2}, use_global_device_ids=true | all-gather | bytes 76032 | tf_op jit(solution)/shard_map/all_gather | solution.py:61
  9.6 1.3 %collective-permute-start = (f32[3,33,128]{2,1,0:T(8,128)S(1)}, f32[3,33,128]{2,1,0:T(8,128)S(1)}, u32[]{:S(2)}, u32[]{:S(2)}) collective-permute-start(f32[3,33,128]{2,1,0:T(8,128)S(1)} %copy.17), channel_id=1, source_target_pairs={{0,8},{8,0},{2,10},{10,2},{4,12},{12,4},{6,14},{14,6},{16,24},{24,... | collective-permute-start | bytes 152072 | tf_op jit(solution)/shard_map/ppermute | solution.py:18
  11.0 0.8 %maximum_select_fusion.1 = f32[3,128]{1,0:T(4,128)S(1)} fusion(f32[3,64]{1,0:T(4,128)} %param.3, f32[3,64]{1,0:T(4,128)S(1)} %collective-permute-done.2, pred[]{:T(512)S(6)} %eq.29), kind=kLoop, calls=%fused_computation.68 | loop fusion | flops 1152 | bytes 3073 | tf_op jit(solution)/shard_map/jit(_where)/select_n | solution.py:69
  11.8 1.2 %collective-permute-start.3 = (f32[3,128]{1,0:T(4,128)S(1)}, f32[3,128]{1,0:T(4,128)S(1)}, u32[]{:S(2)}, u32[]{:S(2)}) collective-permute-start(f32[3,128]{1,0:T(4,128)S(1)} %maximum_select_fusion.1), channel_id=1, source_target_pairs={{0,4},{4,0},{2,6},{6,2},{8,12},{12,8},{10,14},{14,10},{16,20},{20,... | collective-permute-start | bytes 4616 | tf_op jit(solution)/shard_map/ppermute | solution.py:18
  13.1 2.4 %collective-permute-start.1 = (f32[3,33,256]{2,1,0:T(8,128)S(1)}, f32[3,33,256]{2,1,0:T(8,128)S(1)}, u32[]{:S(2)}, u32[]{:S(2)}) collective-permute-start(f32[3,33,256]{2,1,0:T(8,128)S(1)} %pad_maximum_fusion.2), channel_id=1, source_target_pairs={{0,16},{16,0},{2,18},{18,2},{4,20},{20,4},{6,22},{22,6},{8,24},{24... | collective-permute-start | bytes 304136 | tf_op jit(solution)/shard_map/ppermute | solution.py:18
  15.5 4.4 %collective-permute-done.1 = f32[3,33,256]{2,1,0:T(8,128)S(1)} collective-permute-done((f32[3,33,256]{2,1,0:T(8,128)S(1)}, f32[3,33,256]{2,1,0:T(8,128)S(1)}, u32[]{:S(2)}, u32[]{:S(2)}) %collective-permute-start.1) | collective-permute-done | bytes 101408 | tf_op jit(solution)/shard_map/ppermute | solution.py:18
  20.9 4.6 %fusion.16 = f32[32,3,256]{2,0,1:T(8,128)S(1)} fusion(f32[3,256,512]{2,1,0:T(8,128)S(1)} %get-tuple-element.13, f32[3,256,512]{2,1,0:T(8,128)S(1)} %get-tuple-element.12, f32[256,512]{1,0:T(8,128)S(1)} %get-tuple-element.4, f32[3,3]{1,0:T(4,128)S(1)} %fusion.38, f32[3,33,512]{2,1,0:T(8,128)S(1)} %pad_maximum_fusion), kind=kOutput, calls=%fused_computation.20 | convolution fusion | flops 456523776 | bytes 3966976 | tf_op jit(solution)/shard_map/abij,bkj->aki/dot_general | solution.py:40
  25.5 0.6 collective-permute-start.4
  26.1 2.4 %collective-permute-done.4 = f32[3,32,128]{2,1,0:T(8,128)S(1)} collective-permute-done((f32[3,32,128]{2,1,0:T(8,128)S(1)}, f32[3,32,128]{2,1,0:T(8,128)S(1)}, u32[]{:S(2)}, u32[]{:S(2)}) %collective-permute-start.4) | collective-permute-done | bytes 49184 | tf_op jit(solution)/shard_map/ppermute | solution.py:18
  28.6 3.7 %collective-permute-start.5 = (f32[3,32,64]{2,1,0:T(8,128)S(1)}, f32[3,32,64]{2,1,0:T(8,128)S(1)}, u32[]{:S(2)}, u32[]{:S(2)}) collective-permute-start(f32[3,32,64]{2,1,0:T(8,128)S(1)} %constant_dynamic-slice_fusion.1), channel_id=1, source_target_pairs={{0,2},{2,0},{4,6},{6,4},{8,10},{10,8},{12,14},{14,12},{16,18},{18,... | collective-permute-start | bytes 73736 | tf_op jit(solution)/shard_map/ppermute | solution.py:18
  35.7 5.7 %all_gather.7 = f32[3,33,128]{1,0,2:T(4,128)S(1)} all-gather(f32[3,33,64]{1,0,2:T(4,128)S(1)} %copy.18), channel_id=1, replica_groups=mesh['blk'=16,'tile'=2] {'tile'}, dimensions={2}, use_global_device_ids=true | all-gather | bytes 76032 | tf_op jit(solution)/shard_map/all_gather | solution.py:61
  41.8 2.9 %collective-permute-done.6 = f32[3,33,128]{2,1,0:T(8,128)S(1)} collective-permute-done((f32[3,33,128]{2,1,0:T(8,128)S(1)}, f32[3,33,128]{2,1,0:T(8,128)S(1)}, u32[]{:S(2)}, u32[]{:S(2)}) %collective-permute-start.6) | collective-permute-done | bytes 50720 | tf_op jit(solution)/shard_map/ppermute | solution.py:18
  44.7 1.9 %collective-permute-start.7 = (f32[3,33,256]{2,1,0:T(8,128)S(1)}, f32[3,33,256]{2,1,0:T(8,128)S(1)}, u32[]{:S(2)}, u32[]{:S(2)}) collective-permute-start(f32[3,33,256]{2,1,0:T(8,128)S(1)} %pad_maximum_fusion.3), channel_id=1, source_target_pairs={{0,16},{16,0},{2,18},{18,2},{4,20},{20,4},{6,22},{22,6},{8,24},{24... | collective-permute-start | bytes 304136 | tf_op jit(solution)/shard_map/ppermute | solution.py:18
  46.6 4.5 %collective-permute-done.7 = f32[3,33,256]{2,1,0:T(8,128)S(1)} collective-permute-done((f32[3,33,256]{2,1,0:T(8,128)S(1)}, f32[3,33,256]{2,1,0:T(8,128)S(1)}, u32[]{:S(2)}, u32[]{:S(2)}) %collective-permute-start.7) | collective-permute-done | bytes 101408 | tf_op jit(solution)/shard_map/ppermute | solution.py:18
  52.1 4.6 %fusion.19 = f32[32,3,256]{2,0,1:T(8,128)S(1)} fusion(f32[3,256,512]{2,1,0:T(8,128)S(1)} %get-tuple-element.11, f32[3,256,512]{2,1,0:T(8,128)S(1)} %get-tuple-element.10, f32[256,512]{1,0:T(8,128)S(1)} %get-tuple-element.2, f32[3,3]{1,0:T(4,128)S(1)} %fusion.38, f32[3,33,512]{2,1,0:T(8,128)S(1)} %pad_maximum_fusion.1), kind=kOutput, calls=%fused_computation.21 | convolution fusion | flops 456523776 | bytes 3966976 | tf_op jit(solution)/shard_map/abij,bkj->aki/dot_general | solution.py:40
  56.7 1.0 %collective-permute-start.8 = (f32[3,32,128]{2,1,0:T(8,128)S(1)}, f32[3,32,128]{2,1,0:T(8,128)S(1)}, u32[]{:S(2)}, u32[]{:S(2)}) collective-permute-start(f32[3,32,128]{2,1,0:T(8,128)S(1)} %dynamic-slice_bitcast_fusion), channel_id=1, source_target_pairs={{0,4},{4,0},{2,6},{6,2},{8,12},{12,8},{10,14},{14,10},{16,20},{20,... | collective-permute-start | bytes 147464 | tf_op jit(solution)/shard_map/ppermute | solution.py:18
  57.7 2.0 %collective-permute-done.8 = f32[3,32,128]{2,1,0:T(8,128)S(1)} collective-permute-done((f32[3,32,128]{2,1,0:T(8,128)S(1)}, f32[3,32,128]{2,1,0:T(8,128)S(1)}, u32[]{:S(2)}, u32[]{:S(2)}) %collective-permute-start.8) | collective-permute-done | bytes 49184 | tf_op jit(solution)/shard_map/ppermute | solution.py:18
  59.8 4.1 %collective-permute-start.9 = (f32[3,32,64]{2,1,0:T(8,128)S(1)}, f32[3,32,64]{2,1,0:T(8,128)S(1)}, u32[]{:S(2)}, u32[]{:S(2)}) collective-permute-start(f32[3,32,64]{2,1,0:T(8,128)S(1)} %constant_dynamic-slice_fusion), channel_id=1, source_target_pairs={{0,2},{2,0},{4,6},{6,4},{8,10},{10,8},{12,14},{14,12},{16,18},{18,... | collective-permute-start | bytes 73736 | tf_op jit(solution)/shard_map/ppermute | solution.py:18
  63.8 0.7 %multiply_reduce_fusion.2 = (f32[]{:T(128)}, f32[]{:T(128)}) fusion(f32[]{:T(128)} %bitcast.1, f32[]{:T(128)} %bitcast), kind=kLoop, calls=%fused_computation.73 | loop fusion | flops 286 | bytes 16 | tf_op jit(solution)/shard_map/reduce_sum | solution.py:50
  65.9 0.7 multiply_reduce_fusion.4
  67.2 0.7 %fusion.37 = (f32[1,3,32,64]{3,2,1,0:T(8,128)S(1)}, f32[3,32,64]{2,1,0:T(8,128)}) fusion(f32[3,32,64]{2,1,0:T(8,128)S(1)} %collective-permute-done.9, f32[3,32,128]{2,1,0:T(8,128)S(1)} %bitcast_add_fusion, s32[]{:T(128)S(6)} %select_n.117, f32[3,32,64]{2,1,0:T(8,128)S(1)} %copy-done, f32[]{:T(128)} %bitcast.1, f32[3,32,64]{2,1,0:T(8,128)S(1)} %get-tuple-element.7, ...), kind=kLoop, calls=%fused_computation.62 | loop fusion | flops 67584 | bytes 147480 | tf_op jit(solution)/shard_map/stack | solution.py:100
  67.9 0.6 pad_maximum_fusion.4
  (40 shorter events, 3.6 us)
Async XLA Ops:
  0.6 10.4 %collective-permute-start.2 = (f32[3,64]{1,0:T(4,128)}, f32[3,64]{1,0:T(4,128)S(1)}, u32[]{:S(2)}, u32[]{:S(2)}) collective-permute-start(f32[3,64]{1,0:T(4,128)} %param.3), channel_id=1, source_target_pairs={{0,2},{2,0},{4,6},{6,4},{8,10},{10,8},{12,14},{14,12},{16,18},{18,... | collective-permute-start | bytes 2312 | tf_op jit(solution)/shard_map/ppermute | solution.py:18
  9.6 3.4 %collective-permute-start = (f32[3,33,128]{2,1,0:T(8,128)S(1)}, f32[3,33,128]{2,1,0:T(8,128)S(1)}, u32[]{:S(2)}, u32[]{:S(2)}) collective-permute-start(f32[3,33,128]{2,1,0:T(8,128)S(1)} %copy.17), channel_id=1, source_target_pairs={{0,8},{8,0},{2,10},{10,2},{4,12},{12,4},{6,14},{14,6},{16,24},{24,... | collective-permute-start | bytes 152072 | tf_op jit(solution)/shard_map/ppermute | solution.py:18
  11.8 3.6 %collective-permute-start.3 = (f32[3,128]{1,0:T(4,128)S(1)}, f32[3,128]{1,0:T(4,128)S(1)}, u32[]{:S(2)}, u32[]{:S(2)}) collective-permute-start(f32[3,128]{1,0:T(4,128)S(1)} %maximum_select_fusion.1), channel_id=1, source_target_pairs={{0,4},{4,0},{2,6},{6,2},{8,12},{12,8},{10,14},{14,10},{16,20},{20,... | collective-permute-start | bytes 4616 | tf_op jit(solution)/shard_map/ppermute | solution.py:18
  13.1 6.8 %collective-permute-start.1 = (f32[3,33,256]{2,1,0:T(8,128)S(1)}, f32[3,33,256]{2,1,0:T(8,128)S(1)}, u32[]{:S(2)}, u32[]{:S(2)}) collective-permute-start(f32[3,33,256]{2,1,0:T(8,128)S(1)} %pad_maximum_fusion.2), channel_id=1, source_target_pairs={{0,16},{16,0},{2,18},{18,2},{4,20},{20,4},{6,22},{22,6},{8,24},{24... | collective-permute-start | bytes 304136 | tf_op jit(solution)/shard_map/ppermute | solution.py:18
  20.9 11.4 %copy-start.1 = (f32[2]{0:T(128)S(1)}, f32[2]{0:T(128)}, u32[]{:S(2)}) copy-start(f32[2]{0:T(128)} %param.5) | copy-start | bytes 28
  20.9 14.6 %copy-start = (f32[3,32,64]{2,1,0:T(8,128)S(1)}, f32[3,32,64]{2,1,0:T(8,128)}, u32[]{:S(2)}) copy-start(f32[3,32,64]{2,1,0:T(8,128)} %param.4) | copy-start | bytes 73732
  25.5 3.0 %collective-permute-start.4 = (f32[3,32,128]{2,1,0:T(8,128)S(1)}, f32[3,32,128]{2,1,0:T(8,128)S(1)}, u32[]{:S(2)}, u32[]{:S(2)}) collective-permute-start(f32[3,32,128]{2,1,0:T(8,128)S(1)} %dynamic-slice_bitcast_fusion.1), channel_id=1, source_target_pairs={{0,4},{4,0},{2,6},{6,2},{8,12},{12,8},{10,14},{14,10},{16,20},{20,... | collective-permute-start | bytes 147464 | tf_op jit(solution)/shard_map/ppermute | solution.py:18
  28.6 6.9 %collective-permute-start.5 = (f32[3,32,64]{2,1,0:T(8,128)S(1)}, f32[3,32,64]{2,1,0:T(8,128)S(1)}, u32[]{:S(2)}, u32[]{:S(2)}) collective-permute-start(f32[3,32,64]{2,1,0:T(8,128)S(1)} %constant_dynamic-slice_fusion.1), channel_id=1, source_target_pairs={{0,2},{2,0},{4,6},{6,4},{8,10},{10,8},{12,14},{14,12},{16,18},{18,... | collective-permute-start | bytes 73736 | tf_op jit(solution)/shard_map/ppermute | solution.py:18
  41.5 3.1 %collective-permute-start.6 = (f32[3,33,128]{2,1,0:T(8,128)S(1)}, f32[3,33,128]{2,1,0:T(8,128)S(1)}, u32[]{:S(2)}, u32[]{:S(2)}) collective-permute-start(f32[3,33,128]{2,1,0:T(8,128)S(1)} %copy.21), channel_id=1, source_target_pairs={{0,8},{8,0},{2,10},{10,2},{4,12},{12,4},{6,14},{14,6},{16,24},{24,... | collective-permute-start | bytes 152072 | tf_op jit(solution)/shard_map/ppermute | solution.py:18
  44.7 6.4 %collective-permute-start.7 = (f32[3,33,256]{2,1,0:T(8,128)S(1)}, f32[3,33,256]{2,1,0:T(8,128)S(1)}, u32[]{:S(2)}, u32[]{:S(2)}) collective-permute-start(f32[3,33,256]{2,1,0:T(8,128)S(1)} %pad_maximum_fusion.3), channel_id=1, source_target_pairs={{0,16},{16,0},{2,18},{18,2},{4,20},{20,4},{6,22},{22,6},{8,24},{24... | collective-permute-start | bytes 304136 | tf_op jit(solution)/shard_map/ppermute | solution.py:18
  56.7 3.0 %collective-permute-start.8 = (f32[3,32,128]{2,1,0:T(8,128)S(1)}, f32[3,32,128]{2,1,0:T(8,128)S(1)}, u32[]{:S(2)}, u32[]{:S(2)}) collective-permute-start(f32[3,32,128]{2,1,0:T(8,128)S(1)} %dynamic-slice_bitcast_fusion), channel_id=1, source_target_pairs={{0,4},{4,0},{2,6},{6,2},{8,12},{12,8},{10,14},{14,10},{16,20},{20,... | collective-permute-start | bytes 147464 | tf_op jit(solution)/shard_map/ppermute | solution.py:18
  59.8 7.5 %collective-permute-start.9 = (f32[3,32,64]{2,1,0:T(8,128)S(1)}, f32[3,32,64]{2,1,0:T(8,128)S(1)}, u32[]{:S(2)}, u32[]{:S(2)}) collective-permute-start(f32[3,32,64]{2,1,0:T(8,128)S(1)} %constant_dynamic-slice_fusion), channel_id=1, source_target_pairs={{0,2},{2,0},{4,6},{6,4},{8,10},{10,8},{12,14},{14,12},{16,18},{18,... | collective-permute-start | bytes 73736 | tf_op jit(solution)/shard_map/ppermute | solution.py:18
where the time goes:
time: 68.9 us; the launch traced here: 68.6 us
  starting transfers between devices  16.5 us (24%)
  waiting for transfers between devices  16.3 us (24%)
  blocking collectives  12.9 us (19%)
  matrix products  9.13 us (13%)
  other arithmetic  6.43 us (9%)
  between operations  5.42 us (8%)
  local copies, waits for them, and re-layouts  1.92 us (3%)
    ppermute x10, starting transfers between devices, from_partner(): return lax.ppermute(block, axis, route)  16.5 us
    ppermute x10, waiting for transfers between devices, from_partner(): return lax.ppermute(block, axis, route)  16.3 us
    all_gather x2, blocking collectives, grid_product(): sources = lax.all_gather(packed, 'tile', axis=2, tiled=True)  12.9 us
    dot_general x2, matrix products, contract(): jnp.einsum('abij,bkj->aki', tensor, vectors, precision=lax.Precision.HIGH...  9.13 us
    another operation x3, other arithmetic, body(): return (displacement, jnp.stack([first_image, second_image]))  1.45 us
    reduce_sum x2, other arithmetic, weights_from(): jnp.sum(samples * jnp.cos(order * angles))  1.4 us
  transfers between devices with their start and end apart: 10, of which 5 were waited for; matrix products, arithmetic and copies ran while one was open for 7% of the time, Pallas kernels for 0%

commit v1 on v0

--- a/solution.py
+++ b/solution.py
@@ -58,7 +58,8 @@
 def grid_product(packed, positions):
     half_bits = (lax.axis_size("blk").bit_length() - 1) // 2
     block_number = lax.axis_index("blk")
-    sources = lax.all_gather(packed, "tile", axis=2, tiled=True)
+    sent = jnp.stack([packed] * lax.axis_size("tile"))
+    sources = jnp.concatenate(lax.all_to_all(sent, "tile", 0, 0), axis=2)
     for bit_number in range(half_bits, 2 * half_bits):
         partner = from_partner(sources, "blk", bit_number)
         sources = jnp.concatenate([sources, partner], axis=2)

time: 68.9 us -> 72.7 us (1.055)
  starting transfers between devices: 16.5 us -> 25.1 us
  blocking collectives: 12.9 us -> 5.26 us
  local copies, waits for them, and re-layouts: 1.92 us -> 3.51 us
  other arithmetic: 6.43 us -> 7.99 us
    all_gather x2 -> x0, blocking collectives: 12.9 us -> none  [grid_product(): sources = lax.all_gather(packed, 'tile', axis=2, tiled=True)]
    all_to_all x0 -> x1, blocking collectives: none -> 5.26 us  [grid_product(): sources = jnp.concatenate(lax.all_to_all(sent, 'tile', 0, 0), axis=2)]
    ppermute x10, starting transfers between devices: 16.5 us -> 21.2 us  [from_partner(): return lax.ppermute(block, axis, route)]
    all_to_all x0 -> x1, starting transfers between devices: none -> 3.95 us  [grid_product(): sources = jnp.concatenate(lax.all_to_all(sent, 'tile', 0, 0), axis=2)]
    all_to_all x0 -> x2, other arithmetic: none -> 1.59 us  [grid_product(): sources = jnp.concatenate(lax.all_to_all(sent, 'tile', 0, 0), axis=2)]
    unnamed x6 -> x14, local copies, waits for them, and re-layouts: 0.02 us -> 1.15 us
    another operation x0 -> x4, other arithmetic: none -> 0.85 us  [grid_product(): sent = jnp.stack([packed] * lax.axis_size('tile'))]
    concatenate x2 -> x0, other arithmetic: 0.82 us -> none  [mobility(): packed = jnp.concatenate([positions[:, None, :], vectors], axis=1)]
  transfers between devices with their start and end apart: 10 -> 11, of which waited for: 5 -> 7; matrix products, arithmetic and copies ran while one was open for 7% -> 7% of each run, Pallas kernels for 0% -> 0%
where the time goes in v1:
time: 72.7 us; the launch traced here: 72.3 us
  starting transfers between devices  25.1 us (35%)
  waiting for transfers between devices  15.9 us (22%)
  matrix products  9.13 us (13%)
  other arithmetic  7.99 us (11%)
  between operations  5.37 us (7%)
  blocking collectives  5.26 us (7%)
  local copies, waits for them, and re-layouts  3.51 us (5%)
    ppermute x10, starting transfers between devices, from_partner(): return lax.ppermute(block, axis, route)  21.2 us
    ppermute x10, waiting for transfers between devices, from_partner(): return lax.ppermute(block, axis, route)  15.9 us
    dot_general x2, matrix products, contract(): jnp.einsum('abij,bkj->aki', tensor, vectors, precision=lax.Precision.HIGH...  9.13 us
    all_to_all x1, blocking collectives, grid_product(): sources = jnp.concatenate(lax.all_to_all(sent, 'tile', 0, 0), axis=2)  5.26 us
    all_to_all x1, starting transfers between devices, grid_product(): sources = jnp.concatenate(lax.all_to_all(sent, 'tile', 0, 0), axis=2)  3.95 us
    all_to_all x2, other arithmetic, grid_product(): sources = jnp.concatenate(lax.all_to_all(sent, 'tile', 0, 0), axis=2)  1.59 us
  transfers between devices with their start and end apart: 11, of which 7 were waited for; matrix products, arithmetic and copies ran while one was open for 7% of the time, Pallas kernels for 0%

profile of v1, /device:TPU:1, one launch (start us, length us, event | category | flops | bytes accessed | tf_op | source)
XLA Modules:
  0.0 72.3 jit_solution(1774940067765653716)
XLA Ops:
  1.4 0.8 %fusion.36 = f32[1,3,33,64]{3,2,1,0:T(8,128)S(1)} fusion(f32[3,1,64]{2,1,0:T(1,128)S(1)} %broadcast_in_dim.2, f32[3,32,64]{2,1,0:T(8,128)} %param.4), kind=kLoop, calls=%fused_computation.53 | loop fusion | flops 6336 | bytes 50688 | tf_op jit(solution)/shard_map/stack | solution.py:61
  3.0 4.0 %all-to-all-start = ((f32[2,1,6336]{2,1,0:T(1,128)}), f32[2,1,6336]{2,1,0:T(1,128)S(1)}, u32[]{:S(2)}, u32[]{:S(2)}) async-start(f32[2,1,6336]{2,1,0:T(1,128)} %reshape.141), calls=%async_computation | async-start | bytes 102400 | tf_op jit(solution)/shard_map/all_to_all | solution.py:62
  6.9 0.8 %maximum_select_fusion.1 = f32[3,128]{1,0:T(4,128)S(1)} fusion(f32[3,64]{1,0:T(4,128)} %param.3, f32[3,64]{1,0:T(4,128)S(1)} %collective-permute-done.2, pred[]{:T(512)S(6)} %eq.29), kind=kLoop, calls=%fused_computation.74 | loop fusion | flops 1152 | bytes 3073 | tf_op jit(solution)/shard_map/jit(_where)/select_n | solution.py:70
  7.8 2.1 %collective-permute-start.3 = (f32[3,128]{1,0:T(4,128)S(1)}, f32[3,128]{1,0:T(4,128)S(1)}, u32[]{:S(2)}, u32[]{:S(2)}) collective-permute-start(f32[3,128]{1,0:T(4,128)S(1)} %maximum_select_fusion.1), channel_id=1, source_target_pairs={{0,4},{4,0},{2,6},{6,2},{8,12},{12,8},{10,14},{14,10},{16,20},{20,... | collective-permute-start | bytes 4616 | tf_op jit(solution)/shard_map/ppermute | solution.py:18
  9.8 1.1 %collective-permute-done.3 = f32[3,128]{1,0:T(4,128)S(1)} collective-permute-done((f32[3,128]{1,0:T(4,128)S(1)}, f32[3,128]{1,0:T(4,128)S(1)}, u32[]{:S(2)}, u32[]{:S(2)}) %collective-permute-start.3) | collective-permute-done | bytes 1568 | tf_op jit(solution)/shard_map/ppermute | solution.py:18
  11.5 0.8 %reduce = f32[2,6336]{1,0:T(2,128)S(1)} reduce(f32[2,1,6336]{2,1,0:T(1,128)S(1)} %all-to-all-done, f32[]{:T(128)} %broadcast.213), dimensions={1}, to_apply=%all_to_all.6.reduce_sub_computation | reduce | bytes 101380 | tf_op jit(solution)/shard_map/all_to_all | solution.py:62
  12.6 1.7 %collective-permute-start = (f32[3,33,128]{2,1,0:T(8,128)S(1)}, f32[3,33,128]{2,1,0:T(8,128)S(1)}, u32[]{:S(2)}, u32[]{:S(2)}) collective-permute-start(f32[3,33,128]{2,1,0:T(8,128)S(1)} %reshape.134), channel_id=1, source_target_pairs={{0,8},{8,0},{2,10},{10,2},{4,12},{12,4},{6,14},{14,6},{16,24},{24,... | collective-permute-start | bytes 152072 | tf_op jit(solution)/shard_map/ppermute | solution.py:18
  14.3 1.6 %collective-permute-done = f32[3,33,128]{2,1,0:T(8,128)S(1)} collective-permute-done((f32[3,33,128]{2,1,0:T(8,128)S(1)}, f32[3,33,128]{2,1,0:T(8,128)S(1)}, u32[]{:S(2)}, u32[]{:S(2)}) %collective-permute-start) | collective-permute-done | bytes 50720 | tf_op jit(solution)/shard_map/ppermute | solution.py:18
  15.9 2.5 %collective-permute-start.1 = (f32[3,33,256]{2,1,0:T(8,128)S(1)}, f32[3,33,256]{2,1,0:T(8,128)S(1)}, u32[]{:S(2)}, u32[]{:S(2)}) collective-permute-start(f32[3,33,256]{2,1,0:T(8,128)S(1)} %pad_maximum_fusion.1), channel_id=1, source_target_pairs={{0,16},{16,0},{2,18},{18,2},{4,20},{20,4},{6,22},{22,6},{8,24},{24... | collective-permute-start | bytes 304136 | tf_op jit(solution)/shard_map/ppermute | solution.py:18
  18.5 4.0 %collective-permute-done.1 = f32[3,33,256]{2,1,0:T(8,128)S(1)} collective-permute-done((f32[3,33,256]{2,1,0:T(8,128)S(1)}, f32[3,33,256]{2,1,0:T(8,128)S(1)}, u32[]{:S(2)}, u32[]{:S(2)}) %collective-permute-start.1) | collective-permute-done | bytes 101408 | tf_op jit(solution)/shard_map/ppermute | solution.py:18
  23.5 4.6 %fusion.16 = f32[32,3,256]{2,0,1:T(8,128)S(1)} fusion(f32[3,256,512]{2,1,0:T(8,128)S(1)} %get-tuple-element.13, f32[3,256,512]{2,1,0:T(8,128)S(1)} %get-tuple-element.12, f32[256,512]{1,0:T(8,128)S(1)} %get-tuple-element.4, f32[3,3]{1,0:T(4,128)S(1)} %fusion.40, f32[3,33,512]{2,1,0:T(8,128)S(1)} %constant_dynamic-update-slice_fusion), kind=kOutput, calls=%fused_computation.20 | convolution fusion | flops 456523776 | bytes 3966976 | tf_op jit(solution)/shard_map/abij,bkj->aki/dot_general | solution.py:40
  28.1 1.4 %collective-permute-start.4 = (f32[3,32,128]{2,1,0:T(8,128)S(1)}, f32[3,32,128]{2,1,0:T(8,128)S(1)}, u32[]{:S(2)}, u32[]{:S(2)}) collective-permute-start(f32[3,32,128]{2,1,0:T(8,128)S(1)} %dynamic-slice_bitcast_fusion.1), channel_id=1, source_target_pairs={{0,4},{4,0},{2,6},{6,2},{8,12},{12,8},{10,14},{14,10},{16,20},{20,... | collective-permute-start | bytes 147464 | tf_op jit(solution)/shard_map/ppermute | solution.py:18
  29.4 1.7 %collective-permute-done.4 = f32[3,32,128]{2,1,0:T(8,128)S(1)} collective-permute-done((f32[3,32,128]{2,1,0:T(8,128)S(1)}, f32[3,32,128]{2,1,0:T(8,128)S(1)}, u32[]{:S(2)}, u32[]{:S(2)}) %collective-permute-start.4) | collective-permute-done | bytes 49184 | tf_op jit(solution)/shard_map/ppermute | solution.py:18
  31.2 4.0 %collective-permute-start.5 = (f32[3,32,64]{2,1,0:T(8,128)S(1)}, f32[3,32,64]{2,1,0:T(8,128)S(1)}, u32[]{:S(2)}, u32[]{:S(2)}) collective-permute-start(f32[3,32,64]{2,1,0:T(8,128)S(1)} %constant_dynamic-slice_fusion.1), channel_id=1, source_target_pairs={{0,2},{2,0},{4,6},{6,4},{8,10},{10,8},{12,14},{14,12},{16,18},{18,... | collective-permute-start | bytes 73736 | tf_op jit(solution)/shard_map/ppermute | solution.py:18
  38.7 5.3 %all_to_all.10 = f32[2,1,6336]{2,1,0:T(1,128)S(1)} all-to-all(f32[2,1,6336]{2,1,0:T(1,128)S(1)} %reshape.143), channel_id=1, replica_groups=mesh['blk'=16,'tile'=2] {'tile'}, dimensions={0} | all-to-all | bytes 101376 | tf_op jit(solution)/shard_map/all_to_all | solution.py:62
  43.9 0.8 %reduce.1 = f32[2,6336]{1,0:T(2,128)S(1)} reduce(f32[2,1,6336]{2,1,0:T(1,128)S(1)} %all_to_all.10, f32[]{:T(128)} %broadcast.213), dimensions={1}, to_apply=%all_to_all.7.reduce_sub_computation | reduce | bytes 101380 | tf_op jit(solution)/shard_map/all_to_all | solution.py:62
  45.0 0.7 %collective-permute-start.6 = (f32[3,33,128]{2,1,0:T(8,128)S(1)}, f32[3,33,128]{2,1,0:T(8,128)S(1)}, u32[]{:S(2)}, u32[]{:S(2)}) collective-permute-start(f32[3,33,128]{2,1,0:T(8,128)S(1)} %reshape.136), channel_id=1, source_target_pairs={{0,8},{8,0},{2,10},{10,2},{4,12},{12,4},{6,14},{14,6},{16,24},{24,... | collective-permute-start | bytes 152072 | tf_op jit(solution)/shard_map/ppermute | solution.py:18
  45.8 2.4 %collective-permute-done.6 = f32[3,33,128]{2,1,0:T(8,128)S(1)} collective-permute-done((f32[3,33,128]{2,1,0:T(8,128)S(1)}, f32[3,33,128]{2,1,0:T(8,128)S(1)}, u32[]{:S(2)}, u32[]{:S(2)}) %collective-permute-start.6) | collective-permute-done | bytes 50720 | tf_op jit(solution)/shard_map/ppermute | solution.py:18
  48.2 2.4 %collective-permute-start.7 = (f32[3,33,256]{2,1,0:T(8,128)S(1)}, f32[3,33,256]{2,1,0:T(8,128)S(1)}, u32[]{:S(2)}, u32[]{:S(2)}) collective-permute-start(f32[3,33,256]{2,1,0:T(8,128)S(1)} %pad_maximum_fusion.3), channel_id=1, source_target_pairs={{0,16},{16,0},{2,18},{18,2},{4,20},{20,4},{6,22},{22,6},{8,24},{24... | collective-permute-start | bytes 304136 | tf_op jit(solution)/shard_map/ppermute | solution.py:18
  50.6 3.6 %collective-permute-done.7 = f32[3,33,256]{2,1,0:T(8,128)S(1)} collective-permute-done((f32[3,33,256]{2,1,0:T(8,128)S(1)}, f32[3,33,256]{2,1,0:T(8,128)S(1)}, u32[]{:S(2)}, u32[]{:S(2)}) %collective-permute-start.7) | collective-permute-done | bytes 101408 | tf_op jit(solution)/shard_map/ppermute | solution.py:18
  55.2 4.6 %fusion.19 = f32[32,3,256]{2,0,1:T(8,128)S(1)} fusion(f32[3,256,512]{2,1,0:T(8,128)S(1)} %get-tuple-element.11, f32[3,256,512]{2,1,0:T(8,128)S(1)} %get-tuple-element.10, f32[256,512]{1,0:T(8,128)S(1)} %get-tuple-element.2, f32[3,3]{1,0:T(4,128)S(1)} %fusion.40, f32[3,33,512]{2,1,0:T(8,128)S(1)} %constant_dynamic-update-slice_fusion.3), kind=kOutput, calls=%fused_computation.21 | convolution fusion | flops 456523776 | bytes 3966976 | tf_op jit(solution)/shard_map/abij,bkj->aki/dot_general | solution.py:40
  59.8 1.6 %collective-permute-start.8 = (f32[3,32,128]{2,1,0:T(8,128)S(1)}, f32[3,32,128]{2,1,0:T(8,128)S(1)}, u32[]{:S(2)}, u32[]{:S(2)}) collective-permute-start(f32[3,32,128]{2,1,0:T(8,128)S(1)} %dynamic-slice_bitcast_fusion), channel_id=1, source_target_pairs={{0,4},{4,0},{2,6},{6,2},{8,12},{12,8},{10,14},{14,10},{16,20},{20,... | collective-permute-start | bytes 147464 | tf_op jit(solution)/shard_map/ppermute | solution.py:18
  61.4 1.5 %collective-permute-done.8 = f32[3,32,128]{2,1,0:T(8,128)S(1)} collective-permute-done((f32[3,32,128]{2,1,0:T(8,128)S(1)}, f32[3,32,128]{2,1,0:T(8,128)S(1)}, u32[]{:S(2)}, u32[]{:S(2)}) %collective-permute-start.8) | collective-permute-done | bytes 49184 | tf_op jit(solution)/shard_map/ppermute | solution.py:18
  62.9 4.6 %collective-permute-start.9 = (f32[3,32,64]{2,1,0:T(8,128)S(1)}, f32[3,32,64]{2,1,0:T(8,128)S(1)}, u32[]{:S(2)}, u32[]{:S(2)}) collective-permute-start(f32[3,32,64]{2,1,0:T(8,128)S(1)} %constant_dynamic-slice_fusion), channel_id=1, source_target_pairs={{0,2},{2,0},{4,6},{6,4},{8,10},{10,8},{12,14},{14,12},{16,18},{18,... | collective-permute-start | bytes 73736 | tf_op jit(solution)/shard_map/ppermute | solution.py:18
  (54 shorter events, 8.4 us)
Async XLA Ops:
  0.6 6.3 %collective-permute-start.2 = (f32[3,64]{1,0:T(4,128)}, f32[3,64]{1,0:T(4,128)S(1)}, u32[]{:S(2)}, u32[]{:S(2)}) collective-permute-start(f32[3,64]{1,0:T(4,128)} %param.3), channel_id=1, source_target_pairs={{0,2},{2,0},{4,6},{6,4},{8,10},{10,8},{12,14},{14,12},{16,18},{18,... | collective-permute-start | bytes 2312 | tf_op jit(solution)/shard_map/ppermute | solution.py:18
  3.0 8.0 %all-to-all-start = ((f32[2,1,6336]{2,1,0:T(1,128)}), f32[2,1,6336]{2,1,0:T(1,128)S(1)}, u32[]{:S(2)}, u32[]{:S(2)}) async-start(f32[2,1,6336]{2,1,0:T(1,128)} %reshape.141), calls=%async_computation | async-start | bytes 102400 | tf_op jit(solution)/shard_map/all_to_all | solution.py:62
  7.8 3.2 %collective-permute-start.3 = (f32[3,128]{1,0:T(4,128)S(1)}, f32[3,128]{1,0:T(4,128)S(1)}, u32[]{:S(2)}, u32[]{:S(2)}) collective-permute-start(f32[3,128]{1,0:T(4,128)S(1)} %maximum_select_fusion.1), channel_id=1, source_target_pairs={{0,4},{4,0},{2,6},{6,2},{8,12},{12,8},{10,14},{14,10},{16,20},{20,... | collective-permute-start | bytes 4616 | tf_op jit(solution)/shard_map/ppermute | solution.py:18
  12.6 3.4 %collective-permute-start = (f32[3,33,128]{2,1,0:T(8,128)S(1)}, f32[3,33,128]{2,1,0:T(8,128)S(1)}, u32[]{:S(2)}, u32[]{:S(2)}) collective-permute-start(f32[3,33,128]{2,1,0:T(8,128)S(1)} %reshape.134), channel_id=1, source_target_pairs={{0,8},{8,0},{2,10},{10,2},{4,12},{12,4},{6,14},{14,6},{16,24},{24,... | collective-permute-start | bytes 152072 | tf_op jit(solution)/shard_map/ppermute | solution.py:18
  15.9 6.6 %collective-permute-start.1 = (f32[3,33,256]{2,1,0:T(8,128)S(1)}, f32[3,33,256]{2,1,0:T(8,128)S(1)}, u32[]{:S(2)}, u32[]{:S(2)}) collective-permute-start(f32[3,33,256]{2,1,0:T(8,128)S(1)} %pad_maximum_fusion.1), channel_id=1, source_target_pairs={{0,16},{16,0},{2,18},{18,2},{4,20},{20,4},{6,22},{22,6},{8,24},{24... | collective-permute-start | bytes 304136 | tf_op jit(solution)/shard_map/ppermute | solution.py:18
  23.5 11.8 %copy-start.1 = (f32[2]{0:T(128)S(1)}, f32[2]{0:T(128)}, u32[]{:S(2)}) copy-start(f32[2]{0:T(128)} %param.5) | copy-start | bytes 28
  23.5 14.9 %copy-start = (f32[3,32,64]{2,1,0:T(8,128)S(1)}, f32[3,32,64]{2,1,0:T(8,128)}, u32[]{:S(2)}) copy-start(f32[3,32,64]{2,1,0:T(8,128)} %param.4) | copy-start | bytes 73732
  28.1 3.0 %collective-permute-start.4 = (f32[3,32,128]{2,1,0:T(8,128)S(1)}, f32[3,32,128]{2,1,0:T(8,128)S(1)}, u32[]{:S(2)}, u32[]{:S(2)}) collective-permute-start(f32[3,32,128]{2,1,0:T(8,128)S(1)} %dynamic-slice_bitcast_fusion.1), channel_id=1, source_target_pairs={{0,4},{4,0},{2,6},{6,2},{8,12},{12,8},{10,14},{14,10},{16,20},{20,... | collective-permute-start | bytes 147464 | tf_op jit(solution)/shard_map/ppermute | solution.py:18
  31.2 7.2 %collective-permute-start.5 = (f32[3,32,64]{2,1,0:T(8,128)S(1)}, f32[3,32,64]{2,1,0:T(8,128)S(1)}, u32[]{:S(2)}, u32[]{:S(2)}) collective-permute-start(f32[3,32,64]{2,1,0:T(8,128)S(1)} %constant_dynamic-slice_fusion.1), channel_id=1, source_target_pairs={{0,2},{2,0},{4,6},{6,4},{8,10},{10,8},{12,14},{14,12},{16,18},{18,... | collective-permute-start | bytes 73736 | tf_op jit(solution)/shard_map/ppermute | solution.py:18
  45.0 3.1 %collective-permute-start.6 = (f32[3,33,128]{2,1,0:T(8,128)S(1)}, f32[3,33,128]{2,1,0:T(8,128)S(1)}, u32[]{:S(2)}, u32[]{:S(2)}) collective-permute-start(f32[3,33,128]{2,1,0:T(8,128)S(1)} %reshape.136), channel_id=1, source_target_pairs={{0,8},{8,0},{2,10},{10,2},{4,12},{12,4},{6,14},{14,6},{16,24},{24,... | collective-permute-start | bytes 152072 | tf_op jit(solution)/shard_map/ppermute | solution.py:18
  48.2 6.0 %collective-permute-start.7 = (f32[3,33,256]{2,1,0:T(8,128)S(1)}, f32[3,33,256]{2,1,0:T(8,128)S(1)}, u32[]{:S(2)}, u32[]{:S(2)}) collective-permute-start(f32[3,33,256]{2,1,0:T(8,128)S(1)} %pad_maximum_fusion.3), channel_id=1, source_target_pairs={{0,16},{16,0},{2,18},{18,2},{4,20},{20,4},{6,22},{22,6},{8,24},{24... | collective-permute-start | bytes 304136 | tf_op jit(solution)/shard_map/ppermute | solution.py:18
  59.8 3.1 %collective-permute-start.8 = (f32[3,32,128]{2,1,0:T(8,128)S(1)}, f32[3,32,128]{2,1,0:T(8,128)S(1)}, u32[]{:S(2)}, u32[]{:S(2)}) collective-permute-start(f32[3,32,128]{2,1,0:T(8,128)S(1)} %dynamic-slice_bitcast_fusion), channel_id=1, source_target_pairs={{0,4},{4,0},{2,6},{6,2},{8,12},{12,8},{10,14},{14,10},{16,20},{20,... | collective-permute-start | bytes 147464 | tf_op jit(solution)/shard_map/ppermute | solution.py:18
  62.9 8.0 %collective-permute-start.9 = (f32[3,32,64]{2,1,0:T(8,128)S(1)}, f32[3,32,64]{2,1,0:T(8,128)S(1)}, u32[]{:S(2)}, u32[]{:S(2)}) collective-permute-start(f32[3,32,64]{2,1,0:T(8,128)S(1)} %constant_dynamic-slice_fusion), channel_id=1, source_target_pairs={{0,2},{2,0},{4,6},{6,4},{8,10},{10,8},{12,14},{14,12},{16,18},{18,... | collective-permute-start | bytes 73736 | tf_op jit(solution)/shard_map/ppermute | solution.py:18
